TPU v7x, 32 devices: a whole 2x2x4 slice. The times are simulated.
32 devices in a mesh: group: 8 (over y, x, core), section: 4 (over z).
Axes of the slice: x: 2, y: 2, z: 4, core: 2. Of those that a mesh axis runs over, the one named last changes fastest.
Arguments:
- columns: float32 [8, 8, 16, 8192], P('group', None, None, 'section'), may hold values from -6 to 6
- vectors: bfloat16 [8, 8, 128, 8192], P('group', None, None, 'section'), may hold values from -0.0625 to 0.0625
- factors: float32 [8, 8, 128, 128], P('group'), as said below
- order: int32 [8], P('group'), may hold values from 4096 to 8192
- blocks: int32 [8], P('group'), may hold values from 1 to 8
- live: int32 [8, 8], P('group'), may hold values from 0 to 16
Outputs:
- result: float32 [8, 8, 16, 8192], P('group', None, None, 'section')
Inputs may be any that keep to these rules, and one draw needn't show every extreme that they name: `factors`: upper triangular, diagonal entries between one half and two, off-diagonal entries small.
All inputs are finite; a program needn't handle non-finite values.
Results may differ from a plain program's by a relative error of at most 0.0003.
Values sent between devices are 32-bit elements; how exact they have to be, the bound alone decides.
No kernel may reach another device: no remote copies, remote signals or barrier semaphores. Data moves between devices by JAX's collectives and lax.ppermute only.
A program may use at most 64 MiB of HBM per device.

v0:
```python
import jax
import jax.numpy as jnp
from jax import lax
from jax.sharding import PartitionSpec as P


def shards(columns, vectors, factors, order, blocks, live):
    count = vectors.shape[1]
    width = vectors.shape[2]
    rows = vectors.shape[3]
    slots = columns.shape[2]
    first_row = lax.axis_index("section") * rows
    inside = (first_row + jnp.arange(rows) < order[0]).astype(jnp.float32)
    basis_all = vectors[0].astype(jnp.float32) * inside[None, None, :]
    active = (jnp.arange(count) < blocks[0]).astype(jnp.float32)
    factor_all = factors[0] * active[:, None, None]
    high = lax.Precision.HIGHEST
    local_correlation = jnp.einsum("jar,jbr->jab", basis_all[0::2], basis_all[1::2], precision=high)
    correlation_all = lax.psum(local_correlation, "section")
    merged = []
    zeros = jnp.zeros((width, width), jnp.float32)
    for pair in range(count // 2):
        upper_t = factor_all[2 * pair]
        lower_t = factor_all[2 * pair + 1]
        corner = -jnp.dot(
            jnp.dot(upper_t, correlation_all[pair], precision=high), lower_t, precision=high
        )
        top = jnp.concatenate([upper_t, corner], axis=1)
        bottom = jnp.concatenate([zeros, lower_t], axis=1)
        joined = jnp.concatenate([basis_all[2 * pair], basis_all[2 * pair + 1]], axis=0)
        merged.append((joined, jnp.concatenate([top, bottom], axis=0)))
    held = lax.all_to_all(columns[0], "group", split_axis=0, concat_axis=0, tiled=True)
    shape = held.shape
    panel = held.reshape(shape[0] * shape[1], shape[2])
    transform_panel = panel
    for pair in reversed(range(count // 2)):
        joined, factor = merged[pair]
        inner = lax.psum(jnp.dot(transform_panel, joined.T, precision=high), "section")
        scaled = jnp.dot(inner, factor.T, precision=high)
        transform_panel = transform_panel - jnp.dot(scaled, joined, precision=high)
    moved = transform_panel.reshape(shape)
    returned = lax.all_to_all(moved, "group", split_axis=0, concat_axis=0, tiled=True)
    keep = jnp.arange(slots)[None, :] < live[0][:, None]
    return jnp.where(keep[:, :, None], returned, jnp.float32(0.0))[None]


def solution(mesh):
    return jax.shard_map(
        shards,
        mesh=mesh,
        in_specs=(
            P("group", None, None, "section"),
            P("group", None, None, "section"),
            P("group", None, None, None),
            P("group"),
            P("group"),
            P("group", None),
        ),
        out_specs=P("group", None, None, "section"),
        check_vma=False,
    )
```

profile of v0, /device:TPU:0, one launch (start us, length us, event | category | flops | bytes accessed | tf_op | source)
XLA Modules:
  0.0 233.6 jit_solution(4334425276789696389)
XLA Ops:
  6.5 5.2 %all-to-all-start = ((f32[8,16,2048]{2,1,0:T(8,128)}), f32[8,16,2048]{2,1,0:T(8,128)}, u32[]{:S(2)}, u32[]{:S(2)}) async-start(f32[8,16,2048]{2,1,0:T(8,128)} %bitcast.85), calls=%async_computation | async-start | bytes 2097152 | tf_op jit(solution)/shard_map/all_to_all | solution.py:32
  12.4 3.4 %convert_multiply_fusion = f32[8,128,2048]{2,1,0:T(8,128)S(1)} fusion(bf16[1,8,128,2048]{3,2,1,0:T(8,128)(2,1)} %param.7, f32[2048]{0:T(1024)S(1)} %fusion.40), kind=kLoop, calls=%fused_computation | loop fusion | flops 4194304 | bytes 12591104 | tf_op jit(solution)/shard_map/mul | solution.py:14
  15.8 4.7 %fusion = f32[4,128,128]{2,1,0:T(8,128)} fusion(f32[8,128,2048]{2,1,0:T(8,128)S(1)} %convert_multiply_fusion), kind=kOutput, calls=%fused_computation.1 | convolution fusion | flops 1610612736 | bytes 8650752 | tf_op jit(solution)/shard_map/jar,jbr->jab/dot_general | solution.py:18
  21.1 2.5 %slice_bitcast_fusion.1 = (f32[128,2048]{1,0:T(8,128)S(1)}, f32[128,2048]{1,0:T(8,128)S(1)}, f32[128,2048]{1,0:T(8,128)}, f32[128,2048]{1,0:T(8,128)}, f32[128,2...) fusion(f32[8,128,2048]{2,1,0:T(8,128)S(1)} %convert_multiply_fusion), kind=kLoop, calls=%fused_computation.22 | loop fusion | bytes 16777216 | tf_op jit(solution)/shard_map/squeeze | solution.py:30
  23.6 3.6 %all-to-all-done = f32[8,16,2048]{2,1,0:T(8,128)} async-done(((f32[8,16,2048]{2,1,0:T(8,128)}), f32[8,16,2048]{2,1,0:T(8,128)}, u32[]{:S(2)}, u32[]{:S(2)}) %all-to-all-start) | async-done | bytes 1048608 | tf_op jit(solution)/shard_map/all_to_all | solution.py:32
  27.2 4.3 %fusion.7 = f32[128,256]{0,1:T(8,128)} fusion(f32[128,2048]{1,0:T(8,128)} %bitcast.2, f32[128,2048]{1,0:T(8,128)} %get-tuple-element.13, f32[128,2048]{1,0:T(8,128)} %get-tuple-element.14), kind=kOutput, calls=%fused_computation.16 | convolution fusion | flops 805830656 | bytes 3276800 | tf_op jit(solution)/shard_map/dot_general | solution.py:38
  31.6 1.1 bitcast_multiply_fusion
  34.3 34.2 %all-reduce.16.cloned.1.call-done = (f32[128,256]{0,1:T(8,128)}, f32[4,128,128]{2,1,0:T(8,128)}) async-done(((f32[128,256]{0,1:T(8,128)}, f32[4,128,128]{2,1,0:T(8,128)}), (f32[128,256]{0,1:T(8,128)}, f32[4,128,128]{2,1,0:T(8,128)})) %all-reduce.16.cloned.1.call-update) | async-done | bytes 393232 | tf_op jit(solution)/shard_map/psum | solution.py:38
  68.5 1.2 fusion.39
  69.7 1.1 fusion.38
  70.8 1.1 fusion.37
  71.9 1.1 fusion.36
  74.0 1.3 fusion.14
  75.4 2.9 %convolution_subtract_fusion.3 = f32[128,2048]{1,0:T(8,128)S(1)} fusion(f32[128,2048]{1,0:T(8,128)} %bitcast.2, f32[128,256]{1,0:T(8,128)S(1)} %fusion.14, f32[128,2048]{1,0:T(8,128)S(1)} %copy-done.3, f32[128,2048]{1,0:T(8,128)} %get-tuple-element.14), kind=kOutput, calls=%fused_computation.7 | convolution fusion | flops 806092800 | bytes 4325376 | tf_op jit(solution)/shard_map/dot_general | solution.py:40
  79.3 2.9 %fusion.5 = f32[128,256]{1,0:T(8,128)} fusion(f32[128,2048]{1,0:T(8,128)S(1)} %convolution_subtract_fusion.3, f32[128,2048]{1,0:T(8,128)S(1)} %copy-done.1, f32[128,2048]{1,0:T(8,128)S(1)} %copy-done.2), kind=kOutput, calls=%fused_computation.14 | convolution fusion | flops 805830656 | bytes 3276800 | tf_op jit(solution)/shard_map/dot_general | solution.py:38
  82.4 1.7 convolution_negate_fusion.2
  84.1 32.7 %all-reduce.10.cloned.1.call-done = f32[128,256]{1,0:T(8,128)} async-done(((f32[128,256]{1,0:T(8,128)}), f32[128,256]{1,0:T(8,128)}) %all-reduce.10.cloned.1.call-update) | async-done | bytes 131088 | tf_op jit(solution)/shard_map/psum | solution.py:38
  116.7 1.4 fusion.12
  118.1 3.2 %convolution_subtract_fusion.2 = f32[128,2048]{1,0:T(8,128)S(1)} fusion(f32[128,2048]{1,0:T(8,128)} %copy-done.5, f32[128,256]{1,0:T(8,128)S(1)} %fusion.12, f32[128,2048]{1,0:T(8,128)} %get-tuple-element.10, f32[128,2048]{1,0:T(8,128)} %get-tuple-element.11), kind=kOutput, calls=%fused_computation.6 | convolution fusion | flops 806092800 | bytes 4325376 | tf_op jit(solution)/shard_map/dot_general | solution.py:40
  122.3 2.9 %fusion.4 = f32[128,256]{1,0:T(8,128)} fusion(f32[128,2048]{1,0:T(8,128)S(1)} %convolution_subtract_fusion.2, f32[128,2048]{1,0:T(8,128)S(1)} %get-tuple-element.8, f32[128,2048]{1,0:T(8,128)S(1)} %copy-done), kind=kOutput, calls=%fused_computation.13 | convolution fusion | flops 805830656 | bytes 3276800 | tf_op jit(solution)/shard_map/dot_general | solution.py:38
  125.2 1.7 convolution_negate_fusion.1
  126.9 32.7 %all-reduce.12.cloned.1.call-done = f32[128,256]{1,0:T(8,128)} async-done(((f32[128,256]{1,0:T(8,128)}), f32[128,256]{1,0:T(8,128)}) %all-reduce.12.cloned.1.call-update) | async-done | bytes 131088 | tf_op jit(solution)/shard_map/psum | solution.py:38
  159.7 1.3 fusion.10
  161.0 2.8 %convolution_subtract_fusion.1 = f32[128,2048]{1,0:T(8,128)S(1)} fusion(f32[128,2048]{1,0:T(8,128)} %copy-done.6, f32[128,256]{1,0:T(8,128)S(1)} %fusion.10, f32[128,2048]{1,0:T(8,128)S(1)} %get-tuple-element.8, f32[128,2048]{1,0:T(8,128)} %get-tuple-element.9), kind=kOutput, calls=%fused_computation.5 | convolution fusion | flops 806092800 | bytes 4325376 | tf_op jit(solution)/shard_map/dot_general | solution.py:40
  164.7 2.9 %fusion.3 = f32[128,256]{1,0:T(8,128)} fusion(f32[128,2048]{1,0:T(8,128)S(1)} %convolution_subtract_fusion.1, f32[128,2048]{1,0:T(8,128)S(1)} %get-tuple-element.12, f32[128,2048]{1,0:T(8,128)S(1)} %get-tuple-element.7), kind=kOutput, calls=%fused_computation.12 | convolution fusion | flops 805830656 | bytes 3276800 | tf_op jit(solution)/shard_map/dot_general | solution.py:38
  167.6 1.0 convolution_negate_fusion
  168.7 33.4 %all-reduce.14.cloned.1.call-done = f32[128,256]{1,0:T(8,128)} async-done(((f32[128,256]{1,0:T(8,128)}), f32[128,256]{1,0:T(8,128)}) %all-reduce.14.cloned.1.call-update) | async-done | bytes 131088 | tf_op jit(solution)/shard_map/psum | solution.py:38
  202.1 1.3 fusion.8
  203.4 3.4 %convolution_subtract_fusion = f32[128,2048]{1,0:T(8,128)} fusion(f32[128,2048]{1,0:T(8,128)} %copy-done.4, f32[128,256]{1,0:T(8,128)S(1)} %fusion.8, f32[128,2048]{1,0:T(8,128)S(1)} %get-tuple-element.12, f32[128,2048]{1,0:T(8,128)S(1)} %get-tuple-element.7), kind=kOutput, calls=%fused_computation.4 | convolution fusion | flops 806092800 | bytes 4325376 | tf_op jit(solution)/shard_map/dot_general | solution.py:40
  206.9 3.8 %all-to-all-start.1 = ((f32[8,16,2048]{2,1,0:T(8,128)}), f32[8,16,2048]{2,1,0:T(8,128)S(1)}, u32[]{:S(2)}, u32[]{:S(2)}) async-start(f32[8,16,2048]{2,1,0:T(8,128)} %bitcast.28), calls=%async_computation.1 | async-start | bytes 2097152 | tf_op jit(solution)/shard_map/all_to_all | solution.py:42
  210.7 15.3 %all-to-all-done.1 = f32[8,16,2048]{2,1,0:T(8,128)S(1)} async-done(((f32[8,16,2048]{2,1,0:T(8,128)}), f32[8,16,2048]{2,1,0:T(8,128)S(1)}, u32[]{:S(2)}, u32[]{:S(2)}) %all-to-all-start.1) | async-done | bytes 1048608 | tf_op jit(solution)/shard_map/all_to_all | solution.py:42
  226.0 1.1 select_bitcast_fusion
  (33 shorter events, 6.0 us)
Async XLA Ops:
  6.5 20.7 %all-to-all-start = ((f32[8,16,2048]{2,1,0:T(8,128)}), f32[8,16,2048]{2,1,0:T(8,128)}, u32[]{:S(2)}, u32[]{:S(2)}) async-start(f32[8,16,2048]{2,1,0:T(8,128)} %bitcast.85), calls=%async_computation | async-start | bytes 2097152 | tf_op jit(solution)/shard_map/all_to_all | solution.py:32
  11.7 56.8 %all-reduce.16.cloned.1.call-start = ((), (), s32[]{:S(2)}) async-start(), calls=%async_computation.5 | async-start | bytes 786432 | tf_op jit(solution)/shard_map/psum | solution.py:38
  31.5 85.2 %all-reduce.10.cloned.1.call-start = ((), (), s32[]{:S(2)}) async-start(), calls=%async_computation.2 | async-start | bytes 262144 | tf_op jit(solution)/shard_map/psum | solution.py:38
  32.7 0.8 copy-start.7
  68.5 6.8 %copy-start.3 = (f32[128,2048]{1,0:T(8,128)S(1)}, f32[128,2048]{1,0:T(8,128)}, u32[]{:S(2)}) copy-start(f32[128,2048]{1,0:T(8,128)} %get-tuple-element.13) | copy-start | bytes 3145732
  75.3 3.9 %copy-start.1 = (f32[128,2048]{1,0:T(8,128)S(1)}, f32[128,2048]{1,0:T(8,128)}, u32[]{:S(2)}) copy-start(f32[128,2048]{1,0:T(8,128)} %get-tuple-element.10) | copy-start | bytes 3145732
  75.3 3.9 %copy-start.2 = (f32[128,2048]{1,0:T(8,128)S(1)}, f32[128,2048]{1,0:T(8,128)}, u32[]{:S(2)}) copy-start(f32[128,2048]{1,0:T(8,128)} %get-tuple-element.11) | copy-start | bytes 3145732
  78.3 1.0 copy-start.5
  82.2 77.5 %all-reduce.12.cloned.1.call-start = ((), (), s32[]{:S(2)}) async-start(), calls=%async_computation.3 | async-start | bytes 262144 | tf_op jit(solution)/shard_map/psum | solution.py:38
  118.1 4.2 %copy-start = (f32[128,2048]{1,0:T(8,128)S(1)}, f32[128,2048]{1,0:T(8,128)}, u32[]{:S(2)}) copy-start(f32[128,2048]{1,0:T(8,128)} %get-tuple-element.9) | copy-start | bytes 3145732
  121.3 1.0 copy-start.6
  121.3 38.3 %copy-start.8 = (f32[128,128]{1,0:T(8,128)S(1)}, f32[128,128]{1,0:T(8,128)}, u32[]{:S(2)}) copy-start(f32[128,128]{1,0:T(8,128)} %get-tuple-element.18) | copy-start | bytes 196612
  125.2 76.9 %all-reduce.14.cloned.1.call-start = ((), (), s32[]{:S(2)}) async-start(), calls=%async_computation.4 | async-start | bytes 262144 | tf_op jit(solution)/shard_map/psum | solution.py:38
  163.8 1.0 copy-start.4
  206.9 3.8 %copy-start.9 = (s32[1,8]{1,0:T(1,128)S(1)}, s32[1,8]{1,0:T(1,128)}, u32[]{:S(2)}) copy-start(s32[1,8]{1,0:T(1,128)} %param.11) | copy-start | bytes 100
  206.9 19.1 %all-to-all-start.1 = ((f32[8,16,2048]{2,1,0:T(8,128)}), f32[8,16,2048]{2,1,0:T(8,128)S(1)}, u32[]{:S(2)}, u32[]{:S(2)}) async-start(f32[8,16,2048]{2,1,0:T(8,128)} %bitcast.28), calls=%async_computation.1 | async-start | bytes 2097152 | tf_op jit(solution)/shard_map/all_to_all | solution.py:42
Sparse Core Ops, SparseCore 0:
  31.7 36.8 all-reduce.15
  82.3 34.4 all-reduce.9
  125.3 34.2 all-reduce.11
  167.8 34.2 all-reduce.13
where the time goes:
time: 234 us
  waiting for transfers between devices  152 us (65%)
  matrix products  45.1 us (19%)
  between operations  14.7 us (6%)
  starting transfers between devices  9.31 us (4%)
  local copies, waits for them, and re-layouts  6.94 us (3%)
  other arithmetic  5.71 us (2%)
    psum x4, waiting for transfers between devices, shards(): lax.psum(jnp.dot(transform_panel, joined.T, precision=high), 'section')  133 us
    all_to_all x1, waiting for transfers between devices, shards(): lax.all_to_all(moved, 'group', split_axis=0, concat_axis=0, tiled=True)  15.3 us
    dot_general x4, matrix products, shards(): jnp.dot(transform_panel, joined.T, precision=high)  12.9 us
    dot_general x4, matrix products, shards(): transform_panel = transform_panel - jnp.dot(scaled, joined, precision=high)  12.3 us
    dot_general x4, matrix products, shards(): jnp.dot(jnp.dot(upper_t, correlation_all[pair], precision=high), lower_t,...  5.47 us
    dot_general x4, matrix products, shards(): scaled = jnp.dot(inner, factor.T, precision=high)  5.29 us
    all_to_all x1, starting transfers between devices, shards(): lax.all_to_all(columns[0], 'group', split_axis=0, concat_axis=0, tiled=True)  5.2 us
  transfers between devices with their start and end apart: 6, of which 6 were waited for; matrix products, arithmetic and copies ran while one was open for 7% of the time, Pallas kernels for 0%

commit v1 on v0

--- a/solution.py
+++ b/solution.py
@@ -1,7 +1,16 @@
+import functools
 import jax
 import jax.numpy as jnp
 from jax import lax
 from jax.sharding import PartitionSpec as P
+
+
+def ports_lift(m, peer_axis):
+    outcome_arr = jnp.sum(jax.lax.all_gather(m, peer_axis), 0)
+    return outcome_arr
+
+
+report_zones_on_mesh = functools.partial(ports_lift, peer_axis="section")
 
 
 def shards(columns, vectors, factors, order, blocks, live):
@@ -35,7 +44,7 @@
     transform_panel = panel
     for pair in reversed(range(count // 2)):
         joined, factor = merged[pair]
-        inner = lax.psum(jnp.dot(transform_panel, joined.T, precision=high), "section")
+        inner = report_zones_on_mesh(jnp.dot(transform_panel, joined.T, precision=high))
         scaled = jnp.dot(inner, factor.T, precision=high)
         transform_panel = transform_panel - jnp.dot(scaled, joined, precision=high)
     moved = transform_panel.reshape(shape)

time: 234 us -> 194 us (0.83)
  waiting for transfers between devices: 152 us -> 40.1 us
  blocking collectives: 0 us -> 64.5 us
  local copies, waits for them, and re-layouts: 6.94 us -> 13.8 us
  other arithmetic: 5.71 us -> 9.27 us
  matrix products: 45.1 us -> 41.6 us
    psum x4 -> x1, waiting for transfers between devices: 133 us -> 24.8 us  [shards(): correlation_all = lax.psum(local_correlation, 'section')]
    all_gather x0 -> x4, blocking collectives: none -> 64.5 us  [ports_lift(): outcome_arr = jnp.sum(jax.lax.all_gather(m, peer_axis), 0)]
    reduce_sum x0 -> x4, other arithmetic: none -> 4.61 us  [ports_lift(): outcome_arr = jnp.sum(jax.lax.all_gather(m, peer_axis), 0)]
    all_to_all x1, waiting for transfers between devices: 3.61 us -> 0.01 us  [shards(): lax.all_to_all(columns[0], 'group', split_axis=0, concat_axis=0, tiled=True)]
    squeeze x1, local copies, waits for them, and re-layouts: 2.46 us -> 6.05 us  [shards(): basis_all[2 * pair]]
    dot_general x4, matrix products: 12.9 us -> 10.3 us  [shards(): jnp.dot(transform_panel, joined.T, precision=high)]
    unnamed x20 -> x24, local copies, waits for them, and re-layouts: 3.74 us -> 5.01 us
  transfers between devices with their start and end apart: 6 -> 3, of which waited for: 6 -> 2; matrix products, arithmetic and copies ran while one was open for 7% -> 9% of each run, Pallas kernels for 0% -> 0%
where the time goes in v1:
time: 194 us; the launch traced here: 193 us
  blocking collectives  64.5 us (33%)
  matrix products  41.6 us (21%)
  waiting for transfers between devices  40.1 us (21%)
  between operations  15 us (8%)
  local copies, waits for them, and re-layouts  13.8 us (7%)
  other arithmetic  9.27 us (5%)
  starting transfers between devices  8.9 us (5%)
    all_gather x4, blocking collectives, ports_lift(): outcome_arr = jnp.sum(jax.lax.all_gather(m, peer_axis), 0)  64.5 us
    psum x1, waiting for transfers between devices, shards(): correlation_all = lax.psum(local_correlation, 'section')  24.8 us
    all_to_all x1, waiting for transfers between devices, shards(): lax.all_to_all(moved, 'group', split_axis=0, concat_axis=0, tiled=True)  15.2 us
    dot_general x4, matrix products, shards(): transform_panel = transform_panel - jnp.dot(scaled, joined, precision=high)  11.4 us
    dot_general x4, matrix products, shards(): jnp.dot(transform_panel, joined.T, precision=high)  10.3 us
    dot_general x4, matrix products, shards(): jnp.dot(jnp.dot(upper_t, correlation_all[pair], precision=high), lower_t,...  6.68 us
    squeeze x1, local copies, waits for them, and re-layouts, shards(): basis_all[2 * pair]  6.05 us
    all_to_all x1, starting transfers between devices, shards(): lax.all_to_all(columns[0], 'group', split_axis=0, concat_axis=0, tiled=True)  5.21 us
  transfers between devices with their start and end apart: 3, of which 2 were waited for; matrix products, arithmetic and copies ran while one was open for 9% of the time, Pallas kernels for 0%

profile of v1, /device:TPU:0, one launch (start us, length us, event | category | flops | bytes accessed | tf_op | source)
XLA Modules:
  0.0 193.2 jit_solution(15461055781918794026)
XLA Ops:
  7.2 3.4 %convert_multiply_fusion = f32[8,128,2048]{2,1,0:T(8,128)S(1)} fusion(bf16[1,8,128,2048]{3,2,1,0:T(8,128)(2,1)} %param.7, f32[2048]{0:T(1024)S(1)} %fusion.40), kind=kLoop, calls=%fused_computation | loop fusion | flops 4194304 | bytes 12591104 | tf_op jit(solution)/shard_map/mul | solution.py:23
  10.6 3.2 %copy-done = f32[8,128,2048]{2,1,0:T(8,128)} copy-done((f32[8,128,2048]{2,1,0:T(8,128)}, f32[8,128,2048]{2,1,0:T(8,128)S(1)}, u32[]{:S(2)}) %copy-start) | copy-done | bytes 8388632
  13.8 4.7 %fusion = f32[4,128,128]{2,1,0:T(8,128)} fusion(f32[8,128,2048]{2,1,0:T(8,128)S(1)} %convert_multiply_fusion), kind=kOutput, calls=%fused_computation.1 | convolution fusion | flops 1610612736 | bytes 8650752 | tf_op jit(solution)/shard_map/jar,jbr->jab/dot_general | solution.py:27
  18.5 5.2 %all-to-all-start = ((f32[8,16,2048]{2,1,0:T(8,128)}), f32[8,16,2048]{2,1,0:T(8,128)}, u32[]{:S(2)}, u32[]{:S(2)}) async-start(f32[8,16,2048]{2,1,0:T(8,128)} %bitcast.1), calls=%async_computation | async-start | bytes 2097152 | tf_op jit(solution)/shard_map/all_to_all | solution.py:41
  23.7 6.1 %slice_bitcast_fusion.1 = (f32[128,2048]{1,0:T(8,128)S(1)}, f32[128,2048]{1,0:T(8,128)S(1)}, f32[128,2048]{1,0:T(8,128)}, f32[128,2048]{1,0:T(8,128)}, f32[128,2...) fusion(f32[8,128,2048]{2,1,0:T(8,128)} %copy-done), kind=kLoop, calls=%fused_computation.22 | loop fusion | bytes 16777216 | tf_op jit(solution)/shard_map/squeeze | solution.py:39
  32.1 24.8 %all-reduce.6.cloned.1.call-done = f32[4,128,128]{2,1,0:T(8,128)} async-done(((f32[4,128,128]{2,1,0:T(8,128)}), f32[4,128,128]{2,1,0:T(8,128)}) %all-reduce.6.cloned.1.call-update) | async-done | bytes 262160 | tf_op jit(solution)/shard_map/psum | solution.py:28
  58.0 1.7 convolution_negate_fusion.3
  60.7 1.7 convolution_negate_fusion.2
  63.5 1.7 convolution_negate_fusion.1
  66.2 1.7 convolution_negate_fusion
  67.9 3.6 %fusion.7 = f32[128,256]{0,1:T(8,128)S(1)} fusion(f32[128,2048]{1,0:T(8,128)} %bitcast.2, f32[128,2048]{1,0:T(8,128)} %get-tuple-element.11, f32[128,2048]{1,0:T(8,128)} %get-tuple-element.12), kind=kOutput, calls=%fused_computation.16 | convolution fusion | flops 805830656 | bytes 3276800 | tf_op jit(solution)/shard_map/dot_general | solution.py:47
  71.6 16.9 %all-gather = f32[512,256]{0,1:T(8,128)} all-gather(f32[128,256]{0,1:T(8,128)S(1)} %fusion.7), channel_id=2, replica_groups=mesh['group'=8,'section'=4] {'section'}, dimensions={0}, use_global_device_ids=true | all-gather | bytes 655360 | tf_op jit(solution)/shard_map/all_gather | solution.py:9
  88.5 2.0 %reshape.46 = f32[4,128,256]{1,0,2:T(4,128)} reshape(f32[512,256]{0,1:T(8,128)} %all-gather) | data formatting | bytes 1048576 | tf_op jit(solution)/shard_map/all_gather | solution.py:9
  90.5 1.4 reduce_sum.36
  91.9 1.3 fusion.14
  93.2 3.2 %convolution_subtract_fusion.3 = f32[128,2048]{1,0:T(8,128)S(1)} fusion(f32[128,2048]{1,0:T(8,128)} %bitcast.2, f32[128,256]{1,0:T(8,128)S(1)} %fusion.14, f32[128,2048]{1,0:T(8,128)} %get-tuple-element.11, f32[128,2048]{1,0:T(8,128)} %get-tuple-element.12), kind=kOutput, calls=%fused_computation.7 | convolution fusion | flops 806092800 | bytes 4325376 | tf_op jit(solution)/shard_map/dot_general | solution.py:49
  96.5 2.2 %fusion.5 = f32[128,256]{1,0:T(8,128)S(1)} fusion(f32[128,2048]{1,0:T(8,128)S(1)} %convolution_subtract_fusion.3, f32[128,2048]{1,0:T(8,128)S(1)} %copy-done.2, f32[128,2048]{1,0:T(8,128)S(1)} %copy-done.3), kind=kOutput, calls=%fused_computation.14 | convolution fusion | flops 805830656 | bytes 3276800 | tf_op jit(solution)/shard_map/dot_general | solution.py:47
  98.7 16.6 %all-gather.1 = f32[512,256]{1,0:T(8,128)} all-gather(f32[128,256]{1,0:T(8,128)S(1)} %fusion.5), channel_id=3, replica_groups=mesh['group'=8,'section'=4] {'section'}, dimensions={0}, use_global_device_ids=true | all-gather | bytes 655360 | tf_op jit(solution)/shard_map/all_gather | solution.py:9
  115.3 1.1 reduce_sum.37
  116.4 1.3 fusion.12
  117.7 3.2 %convolution_subtract_fusion.2 = f32[128,2048]{1,0:T(8,128)S(1)} fusion(f32[128,2048]{1,0:T(8,128)} %copy-done.6, f32[128,256]{1,0:T(8,128)S(1)} %fusion.12, f32[128,2048]{1,0:T(8,128)} %get-tuple-element.8, f32[128,2048]{1,0:T(8,128)} %get-tuple-element.9), kind=kOutput, calls=%fused_computation.6 | convolution fusion | flops 806092800 | bytes 4325376 | tf_op jit(solution)/shard_map/dot_general | solution.py:49
  120.9 2.2 %fusion.4 = f32[128,256]{1,0:T(8,128)S(1)} fusion(f32[128,2048]{1,0:T(8,128)S(1)} %convolution_subtract_fusion.2, f32[128,2048]{1,0:T(8,128)S(1)} %get-tuple-element.6, f32[128,2048]{1,0:T(8,128)S(1)} %copy-done.1), kind=kOutput, calls=%fused_computation.13 | convolution fusion | flops 805830656 | bytes 3276800 | tf_op jit(solution)/shard_map/dot_general | solution.py:47
  123.2 15.4 %all-gather.2 = f32[512,256]{1,0:T(8,128)} all-gather(f32[128,256]{1,0:T(8,128)S(1)} %fusion.4), channel_id=4, replica_groups=mesh['group'=8,'section'=4] {'section'}, dimensions={0}, use_global_device_ids=true | all-gather | bytes 655360 | tf_op jit(solution)/shard_map/all_gather | solution.py:9
  138.6 1.1 reduce_sum.38
  139.7 1.2 fusion.10
  140.9 2.8 %convolution_subtract_fusion.1 = f32[128,2048]{1,0:T(8,128)S(1)} fusion(f32[128,2048]{1,0:T(8,128)} %copy-done.7, f32[128,256]{1,0:T(8,128)S(1)} %fusion.10, f32[128,2048]{1,0:T(8,128)S(1)} %get-tuple-element.6, f32[128,2048]{1,0:T(8,128)} %get-tuple-element.7), kind=kOutput, calls=%fused_computation.5 | convolution fusion | flops 806092800 | bytes 4325376 | tf_op jit(solution)/shard_map/dot_general | solution.py:49
  144.7 2.2 %fusion.3 = f32[128,256]{1,0:T(8,128)S(1)} fusion(f32[128,2048]{1,0:T(8,128)S(1)} %convolution_subtract_fusion.1, f32[128,2048]{1,0:T(8,128)S(1)} %get-tuple-element.10, f32[128,2048]{1,0:T(8,128)S(1)} %get-tuple-element.5), kind=kOutput, calls=%fused_computation.12 | convolution fusion | flops 805830656 | bytes 3276800 | tf_op jit(solution)/shard_map/dot_general | solution.py:47
  146.9 15.5 %all-gather.3 = f32[512,256]{1,0:T(8,128)} all-gather(f32[128,256]{1,0:T(8,128)S(1)} %fusion.3), channel_id=5, replica_groups=mesh['group'=8,'section'=4] {'section'}, dimensions={0}, use_global_device_ids=true | all-gather | bytes 655360 | tf_op jit(solution)/shard_map/all_gather | solution.py:9
  164.0 2.2 %convolution_subtract_fusion = f32[128,2048]{1,0:T(8,128)} fusion(f32[128,2048]{1,0:T(8,128)S(1)} %copy-done.5, f32[128,256]{1,0:T(8,128)S(1)} %fusion.8, f32[128,2048]{1,0:T(8,128)S(1)} %get-tuple-element.10, f32[128,2048]{1,0:T(8,128)S(1)} %get-tuple-element.5), kind=kOutput, calls=%fused_computation.4 | convolution fusion | flops 806092800 | bytes 4325376 | tf_op jit(solution)/shard_map/dot_general | solution.py:49
  166.2 3.7 %all-to-all-start.1 = ((f32[8,16,2048]{2,1,0:T(8,128)}), f32[8,16,2048]{2,1,0:T(8,128)S(1)}, u32[]{:S(2)}, u32[]{:S(2)}) async-start(f32[8,16,2048]{2,1,0:T(8,128)} %bitcast.90), calls=%async_computation.1 | async-start | bytes 2097152 | tf_op jit(solution)/shard_map/all_to_all | solution.py:51
  170.0 15.2 %all-to-all-done.1 = f32[8,16,2048]{2,1,0:T(8,128)S(1)} async-done(((f32[8,16,2048]{2,1,0:T(8,128)}), f32[8,16,2048]{2,1,0:T(8,128)S(1)}, u32[]{:S(2)}, u32[]{:S(2)}) %all-to-all-start.1) | async-done | bytes 1048608 | tf_op jit(solution)/shard_map/all_to_all | solution.py:51
  185.2 1.1 select_bitcast_fusion
  (37 shorter events, 8.5 us)
Async XLA Ops:
  6.5 50.4 %all-reduce.6.cloned.1.call-start = ((), (), s32[]{:S(2)}) async-start(), calls=%async_computation.2 | async-start | bytes 524288 | tf_op jit(solution)/shard_map/psum | solution.py:28
  10.6 3.2 %copy-start = (f32[8,128,2048]{2,1,0:T(8,128)}, f32[8,128,2048]{2,1,0:T(8,128)S(1)}, u32[]{:S(2)}) copy-start(f32[8,128,2048]{2,1,0:T(8,128)S(1)} %convert_multiply_fusion) | copy-start | bytes 25165828
  18.5 49.4 %all-to-all-start = ((f32[8,16,2048]{2,1,0:T(8,128)}), f32[8,16,2048]{2,1,0:T(8,128)}, u32[]{:S(2)}, u32[]{:S(2)}) async-start(f32[8,16,2048]{2,1,0:T(8,128)} %bitcast.1), calls=%async_computation | async-start | bytes 2097152 | tf_op jit(solution)/shard_map/all_to_all | solution.py:41
  23.7 6.7 %copy-start.9 = (f32[1,8,128,128]{3,2,1,0:T(8,128)S(1)}, f32[1,8,128,128]{3,2,1,0:T(8,128)}, u32[]{:S(2)}) copy-start(f32[1,8,128,128]{3,2,1,0:T(8,128)} %param.8) | copy-start | bytes 1572868
  30.5 0.8 copy-start.8
  93.2 3.3 %copy-start.2 = (f32[128,2048]{1,0:T(8,128)S(1)}, f32[128,2048]{1,0:T(8,128)}, u32[]{:S(2)}) copy-start(f32[128,2048]{1,0:T(8,128)} %get-tuple-element.8) | copy-start | bytes 3145732
  93.2 3.3 %copy-start.3 = (f32[128,2048]{1,0:T(8,128)S(1)}, f32[128,2048]{1,0:T(8,128)}, u32[]{:S(2)}) copy-start(f32[128,2048]{1,0:T(8,128)} %get-tuple-element.9) | copy-start | bytes 3145732
  96.4 2.3 %copy-start.6 = (f32[128,2048]{1,0:T(8,128)}, f32[128,2048]{1,0:T(8,128)S(1)}, u32[]{:S(2)}) copy-start(f32[128,2048]{1,0:T(8,128)S(1)} %convolution_subtract_fusion.3) | copy-start | bytes 3145732
  117.7 3.2 %copy-start.1 = (f32[128,2048]{1,0:T(8,128)S(1)}, f32[128,2048]{1,0:T(8,128)}, u32[]{:S(2)}) copy-start(f32[128,2048]{1,0:T(8,128)} %get-tuple-element.7) | copy-start | bytes 3145732
  120.9 2.2 %copy-start.7 = (f32[128,2048]{1,0:T(8,128)}, f32[128,2048]{1,0:T(8,128)S(1)}, u32[]{:S(2)}) copy-start(f32[128,2048]{1,0:T(8,128)S(1)} %convolution_subtract_fusion.2) | copy-start | bytes 3145732
  143.7 1.0 copy-start.4
  144.7 18.9 %copy-start.10 = (f32[128,128]{1,0:T(8,128)S(1)}, f32[128,128]{1,0:T(8,128)}, u32[]{:S(2)}) copy-start(f32[128,128]{1,0:T(8,128)} %convolution_negate_fusion) | copy-start | bytes 196612
  146.9 17.1 %copy-start.5 = (f32[128,2048]{1,0:T(8,128)S(1)}, f32[128,2048]{1,0:T(8,128)}, u32[]{:S(2)}) copy-start(f32[128,2048]{1,0:T(8,128)} %copy-done.4) | copy-start | bytes 3145732
  166.2 3.7 %copy-start.11 = (s32[1,8]{1,0:T(1,128)S(1)}, s32[1,8]{1,0:T(1,128)}, u32[]{:S(2)}) copy-start(s32[1,8]{1,0:T(1,128)} %param.11) | copy-start | bytes 100
  166.2 19.0 %all-to-all-start.1 = ((f32[8,16,2048]{2,1,0:T(8,128)}), f32[8,16,2048]{2,1,0:T(8,128)S(1)}, u32[]{:S(2)}, u32[]{:S(2)}) async-start(f32[8,16,2048]{2,1,0:T(8,128)} %bitcast.90), calls=%async_computation.1 | async-start | bytes 2097152 | tf_op jit(solution)/shard_map/all_to_all | solution.py:51
Sparse Core Ops, SparseCore 0:
  18.6 38.2 all-reduce.5
